TPU v7x, 32 devices: a whole 2x2x4 slice. The times are simulated.
32 devices in a mesh: py: 2 (over y), px: 4 (over x, core), pz: 4 (over z).
Axes of the slice: x: 2, y: 2, z: 4, core: 2. Of those that a mesh axis runs over, the one named last changes fastest.
Arguments:
- tracer: float32 [32, 512, 32, 128], P('py', 'px', 'pz'), may hold values from 0.2 to 1.8
- conductance: float32 [32, 512, 32, 128], P('py', 'px', 'pz'), may hold values from 0.03 to 0.15
- source: float32 [32, 512, 32, 128], P('py', 'px', 'pz'), may hold values from -0.2 to 0.2
Outputs:
- potential: float32 [32, 512, 32, 128], P('py', 'px', 'pz')
- tracer_end: float32 [32, 512, 32, 128], P('py', 'px', 'pz')
All inputs are finite; a program needn't handle non-finite values.
Results may differ from a plain program's by a relative error of at most 0.00002.
Values sent between devices are 32-bit elements; how exact they have to be, the bound alone decides.
A program may use at most 320 MiB of HBM per device.

v0:
```python
import functools

import jax
import jax.numpy as jnp
from jax import lax
from jax.experimental import pallas as pl
from jax.experimental.pallas import tpu as pltpu
from jax.sharding import PartitionSpec as P

STEPS = 4
MESH = pl.DeviceIdType.MESH


def chunks_of(cells):
    for parts in (8, 4, 2):
        if cells % (8 * parts) == 0:
            return parts
    raise ValueError("x extent")


def evolve(
    counts, parts, deep, tracer, conductance, source, end, below,
    field, coeff, gain, zhalo, yhalo, xhalo, zface, entering, leaving,
    load_sem, zsend, zrecv, ysend, yrecv, xsend, xrecv, psend, precv,
):
    rows_y, all_rows, members = tracer.shape
    cells = all_rows // deep
    wide = cells // parts
    rows = wide * deep
    halves = psend.shape[1]
    count = dict(zip(("py", "px", "pz"), counts))
    mine = {axis: lax.axis_index(axis) for axis in count}
    after = {axis: lax.rem(mine[axis] + 1, count[axis]) for axis in count}
    before = {axis: lax.rem(mine[axis] + count[axis] - 1, count[axis]) for axis in count}
    body_y = pl.ds(1, rows_y)

    def span(c):
        return pl.ds(pl.multiple_of(c * rows, 8), rows)

    def inner(c):
        return pl.ds(pl.multiple_of(c * rows + deep, 8), rows)

    def cell_span(c):
        return pl.ds(pl.multiple_of(c * wide, 8), wide)

    def load(which, c):
        hbm, dst = (
            (tracer, field.at[0, body_y, inner(c), :]),
            (conductance, coeff.at[:, span(c), :]),
            (source, gain.at[:, span(c), :]),
        )[which]
        return pltpu.make_async_copy(hbm.at[:, span(c), :], dst, load_sem.at[which, c])

    def remote(src, dst, send, recv, axis, target):
        return pltpu.make_async_remote_copy(
            src_ref=src, dst_ref=dst, send_sem=send, recv_sem=recv,
            device_id={axis: target}, device_id_type=MESH,
        )

    def z_copy(t, side, c):
        return remote(
            zface.at[lax.rem(t, 2), side, :, cell_span(c), :],
            zhalo.at[t, side, :, cell_span(c), :],
            zsend.at[t, side, c], zrecv.at[t, side, c],
            "pz", (after, before)[side]["pz"],
        )

    def y_copy(t, side, c):
        return remote(
            field.at[lax.rem(t, 2), (rows_y, 1)[side], inner(c), :],
            yhalo.at[t, side, span(c), :],
            ysend.at[t, side, c], yrecv.at[t, side, c],
            "py", (after, before)[side]["py"],
        )

    def x_copy(t, side):
        return remote(
            field.at[lax.rem(t, 2), body_y, pl.ds((all_rows, deep)[side], deep), :],
            xhalo.at[t, side],
            xsend.at[t, side], xrecv.at[t, side],
            "px", (after, before)[side]["px"],
        )

    def part_y(h):
        return pl.ds(h * (rows_y // halves), rows_y // halves)

    def prefix_copy(c, h):
        return remote(
            leaving.at[part_y(h), cell_span(c), :], entering.at[part_y(h), cell_span(c), :],
            psend.at[c, h], precv.at[c, h], "pz", after["pz"],
        )

    def send_faces(t, c):
        for side in (0, 1):
            z_copy(t, side, c).start()
            y_copy(t, side, c).start()

        @pl.when(c == 0)
        def _():
            x_copy(t, 1).start()

        @pl.when(c == parts - 1)
        def _():
            x_copy(t, 0).start()

    def face_of(p, y, c, z):
        return field[p, y, pl.ds(c * rows + deep + z, wide, stride=deep), :]

    def keep_z_faces(p, y, c):
        zface[p, 0, y, cell_span(c), :] = face_of(p, y + 1, c, deep - 1)
        zface[p, 1, y, cell_span(c), :] = face_of(p, y + 1, c, 0)

    def each_chunk(work):
        def run(c, carry):
            work(c)
            return carry

        lax.fori_loop(0, parts, run, 0)

    load(0, 0).start()
    load(0, 1).start()

    barrier = pltpu.get_barrier_semaphore()
    for axis in count:
        for target in (after[axis], before[axis]):
            pl.semaphore_signal(barrier, inc=1, device_id={axis: target}, device_id_type=MESH)
    pl.semaphore_wait(barrier, 6)

    def first_faces(c):
        load(0, c).wait()

        @pl.when(c < parts - 2)
        def _():
            load(0, c + 2).start()

        def row(y, carry):
            keep_z_faces(0, y, c)
            return carry

        lax.fori_loop(0, rows_y, row, 0)
        send_faces(0, c)
        load(1, c).start()
        load(2, c).start()

    each_chunk(first_faces)

    def wait_sent(t, c):
        for side in (0, 1):
            z_copy(t, side, c).wait_send()
            y_copy(t, side, c).wait_send()

        @pl.when(c == 0)
        def _():
            x_copy(t, 1).wait_send()

        @pl.when(c == parts - 1)
        def _():
            x_copy(t, 0).wait_send()

    level = lax.broadcasted_iota(jnp.int32, (wide, deep, members), 1)

    def step(t, carry):
        old, new = lax.rem(t, 2), lax.rem(t + 1, 2)

        def chunk(c):
            @pl.when(t == 0)
            def _():
                load(1, c).wait()
                load(2, c).wait()

            @pl.when(t > 0)
            def _():
                wait_sent(t - 1, c)

            for side in (0, 1):
                z_copy(t, side, c).wait_recv()
                y_copy(t, side, c).wait_recv()
                field[old, (0, rows_y + 1)[side], inner(c), :] = yhalo[t, side, span(c), :]

            @pl.when(c == 0)
            def _():
                x_copy(t, 0).wait_recv()
                field[old, body_y, pl.ds(0, deep), :] = xhalo[t, 0]

            @pl.when(c == parts - 1)
            def _():
                x_copy(t, 1).wait_recv()
                field[old, body_y, pl.ds(all_rows + deep, deep), :] = xhalo[t, 1]

            def row(y, carry):
                def at(dy, dx):
                    start = pl.multiple_of(c * rows + deep + dx * deep, 8)
                    return field[old, y + 1 + dy, pl.ds(start, rows), :]

                def tall(values):
                    return jnp.broadcast_to(values[:, None, :], (wide, deep, members))

                middle = at(0, 0)
                block = middle.reshape(wide, deep, members)
                first = tall(zhalo[t, 0, y, cell_span(c), :])
                last = tall(zhalo[t, 1, y, cell_span(c), :])
                lower = jnp.where(level == 0, first, pltpu.roll(block, 1, 1))
                upper = jnp.where(level == deep - 1, last, pltpu.roll(block, deep - 1, 1))
                along = (lower + upper).reshape(rows, members)
                spread = at(-1, 0) + at(1, 0) + at(0, -1) + at(0, 1) + along - 6.0 * middle
                field[new, y + 1, inner(c), :] = (
                    middle + coeff[y, span(c), :] * spread + gain[y, span(c), :]
                )
                return carry

            lax.fori_loop(0, rows_y, row, 0)

            @pl.when(t < STEPS - 1)
            def _():
                def faces(y, carry):
                    keep_z_faces(new, y, c)
                    return carry

                lax.fori_loop(0, rows_y, faces, 0)
                send_faces(t + 1, c)

            @pl.when(t == STEPS - 1)
            def _():
                def totals(y, carry):
                    end[y, span(c), :] = field[new, y + 1, inner(c), :]
                    total = face_of(new, y + 1, c, 0)
                    for z in range(1, deep):
                        total = total + face_of(new, y + 1, c, z)
                    leaving[y, cell_span(c), :] = total
                    return carry

                lax.fori_loop(0, rows_y, totals, 0)

                @pl.when(mine["pz"] == 0)
                def _():
                    entering[:, cell_span(c), :] = jnp.zeros((rows_y, wide, members), jnp.float32)
                    for h in range(halves):
                        prefix_copy(c, h).start()

        each_chunk(chunk)
        return carry

    lax.fori_loop(0, STEPS, step, 0)

    @pl.when(mine["pz"] > 0)
    def _():
        def pass_on(c):
            for h in range(halves):
                prefix_copy(c, h).wait_recv()

                @pl.when(mine["pz"] < count["pz"] - 1)
                def _():
                    leaving[part_y(h), cell_span(c), :] += entering[part_y(h), cell_span(c), :]
                    prefix_copy(c, h).start()

        each_chunk(pass_on)

    def keep_below(y, carry):
        below[y] = entering[y]
        return carry

    lax.fori_loop(0, rows_y, keep_below, 0)

    def finish(c):
        wait_sent(STEPS - 1, c)

        @pl.when(mine["pz"] < count["pz"] - 1)
        def _():
            for h in range(halves):
                prefix_copy(c, h).wait_send()

    each_chunk(finish)


def sums(depth, end, below, potential, tracer_end, ready, end_sem, sum_sem):
    rows_y, all_rows, members = end.shape
    cells = below.shape[1]
    deep = all_rows // cells
    slots = ready.shape[0]
    level = lax.broadcasted_iota(jnp.int32, (cells, deep, members), 1)
    whole = pltpu.make_async_copy(end, tracer_end, end_sem)
    whole.start()

    def store(y):
        slot = lax.rem(y, slots)
        return pltpu.make_async_copy(ready.at[slot], potential.at[y], sum_sem.at[slot])

    def row(y, carry):
        @pl.when(y >= slots)
        def _():
            store(y - slots).wait()

        block = end[y].reshape(cells, deep, members)
        reach = 1
        while reach < deep:
            block = block + jnp.where(level >= reach, pltpu.roll(block, reach, 1), 0.0)
            reach *= 2
        block = block + jnp.broadcast_to(below[y][:, None, :], block.shape)
        ready[lax.rem(y, slots)] = (block / depth).reshape(all_rows, members)
        store(y).start()
        return carry

    lax.fori_loop(0, rows_y, row, 0)

    def drain(y, carry):
        store(y).wait()
        return carry

    lax.fori_loop(rows_y - slots, rows_y, drain, 0)
    whole.wait()


def on_device(counts, tracer, conductance, source):
    shape = tracer.shape
    rows_y, cells, deep, members = shape
    parts = chunks_of(cells)
    rows = cells * deep
    halves = next((h for h in (4, 2) if rows_y % h == 0), 1)
    flat = (rows_y, rows, members)
    anywhere = pl.BlockSpec(memory_space=pl.ANY)
    near = pl.BlockSpec(memory_space=pltpu.VMEM)
    f32 = jnp.float32
    dma = pltpu.SemaphoreType.DMA
    end, below = pl.pallas_call(
        functools.partial(evolve, counts, parts, deep),
        out_shape=(
            pltpu.VMEM(flat, f32),
            pltpu.VMEM((rows_y, cells, members), f32),
        ),
        in_specs=[anywhere] * 3,
        out_specs=(near, near),
        scratch_shapes=[
            pltpu.VMEM((2, rows_y + 2, rows + 2 * deep, members), f32),
            pltpu.VMEM(flat, f32),
            pltpu.VMEM(flat, f32),
            pltpu.VMEM((STEPS, 2, rows_y, cells, members), f32),
            pltpu.VMEM((STEPS, 2, rows, members), f32),
            pltpu.VMEM((STEPS, 2, rows_y, deep, members), f32),
            pltpu.VMEM((2, 2, rows_y, cells, members), f32),
            pltpu.VMEM((rows_y, cells, members), f32),
            pltpu.VMEM((rows_y, cells, members), f32),
            dma((3, parts)),
            dma((STEPS, 2, parts)), dma((STEPS, 2, parts)),
            dma((STEPS, 2, parts)), dma((STEPS, 2, parts)),
            dma((STEPS, 2)), dma((STEPS, 2)),
            dma((parts, halves)), dma((parts, halves)),
        ],
        compiler_params=pltpu.CompilerParams(
            collective_id=0, has_side_effects=True, vmem_limit_bytes=53 * 1024 * 1024 + 524288
        ),
        name="evolve",
    )(*(array.reshape(flat) for array in (tracer, conductance, source)))
    slots = min(4, rows_y)
    potential, tracer_end = pl.pallas_call(
        functools.partial(sums, deep * counts[2]),
        out_shape=(jax.ShapeDtypeStruct(flat, f32),) * 2,
        in_specs=[near, near],
        out_specs=(anywhere, anywhere),
        scratch_shapes=[pltpu.VMEM((slots, rows, members), f32), dma(()), dma((slots,))],
        compiler_params=pltpu.CompilerParams(vmem_limit_bytes=16 * 1024 * 1024),
        name="sums",
    )(end, below)
    return potential.reshape(shape), tracer_end.reshape(shape)


def solution(mesh):
    placed = P("py", "px", "pz", None)
    counts = tuple(mesh.shape[axis] for axis in ("py", "px", "pz"))
    return jax.shard_map(
        functools.partial(on_device, counts),
        mesh=mesh,
        in_specs=(placed,) * 3,
        out_specs=(placed,) * 2,
        check_vma=False,
    )
```

profile of v0, /device:TPU:24, one launch (start us, length us, event | category | flops | bytes accessed | tf_op | source)
XLA Modules:
  0.0 223.2 jit_solution(1581654713909067731)
XLA Ops:
  0.6 215.1 %evolve.1 = (f32[16,1024,128]{2,1,0:T(8,128)S(1)}, f32[16,128,128]{2,1,0:T(8,128)S(1)}) custom-call(f32[16,1024,128]{2,1,0:T(8,128)} %bitcast.5, f32[16,1024,128]{2,1,0:T(8,128)} %bitcast.6, f32[16,1024,128]{2,1,0:T(8,128)} %bitcast.7), custom_call_target="tpu_custom_call" | custom-call | tf_op jit(solution)/shard_map/evolve/pallas_call | solution.py:324
  215.8 7.4 %sums.1 = (f32[16,1024,128]{2,1,0:T(8,128)}, f32[16,1024,128]{2,1,0:T(8,128)}) custom-call(f32[16,1024,128]{2,1,0:T(8,128)S(1)} %get-tuple-element.6.end, f32[16,128,128]{2,1,0:T(8,128)S(1)} %get-tuple-element.7.below), custom_call_target="tpu_custom_call" | custom-call | tf_op jit(solution)/shard_map/sums/pallas_call | solution.py:354
where the time goes:
time: 223 us
  Pallas kernels  223 us (100%)
    pallas_call x1, Pallas kernels, on_device(): pl.pallas_call(functools.partial(evolve, counts, parts, deep), out_shape=...  215 us
    pallas_call x1, Pallas kernels, on_device(): pl.pallas_call(functools.partial(sums, deep * counts[2]), out_shape=(jax....  7.4 us

commit v1 on v0

v1 whole, which is shorter than its diff:
```python
import functools

import jax
import jax.numpy as jnp
from jax import lax
from jax.experimental import pallas as pl
from jax.experimental.pallas import tpu as pltpu
from jax.sharding import PartitionSpec as P

STEPS = 4
LAST = STEPS - 1
AXES = ("py", "px", "pz")
MESH = pl.DeviceIdType.MESH


def chunks_of(cells):
    for parts in (16, 8, 4, 2):
        if cells % (8 * parts) == 0:
            return parts
    raise ValueError("x extent")


def evolve(
    counts, parts, tracer, conductance, source, end, running,
    field, coeff, gain, zhalo, entering,
    load_sem, zsend, zrecv, ysend, yrecv, xsend, xrecv, psend, precv,
):
    rows_y, cells, deep, members = tracer.shape
    wide = cells // parts
    behind = parts // 2
    scale = 1.0 / (deep * counts[2])
    count = dict(zip(AXES, counts))
    mine = {axis: lax.axis_index(axis) for axis in count}
    after = {axis: lax.rem(mine[axis] + 1, count[axis]) for axis in count}
    before = {axis: lax.rem(mine[axis] + count[axis] - 1, count[axis]) for axis in count}
    lowest = mine["pz"] == 0
    highest = mine["pz"] == count["pz"] - 1
    body_y = pl.ds(1, rows_y)

    def span(c):
        return pl.ds(pl.multiple_of(c * wide, 8), wide)

    def inner(c, shift=0):
        return pl.ds(c * wide + 1 + shift, wide)

    def load(which, c):
        hbm, dst = (
            (tracer, field.at[0, body_y, inner(c)]),
            (conductance, coeff.at[:, span(c)]),
            (source, gain.at[:, span(c)]),
        )[which]
        return pltpu.make_async_copy(hbm.at[:, span(c)], dst, load_sem.at[which, c])

    def remote(src, dst, send, recv, axis, target):
        return pltpu.make_async_remote_copy(
            src_ref=src, dst_ref=dst, send_sem=send, recv_sem=recv,
            device_id={axis: target}, device_id_type=MESH,
        )

    def z_copy(t, side, c):
        p = lax.rem(t, 2)
        return remote(
            field.at[p, body_y, inner(c), (deep - 1, 0)[side]],
            zhalo.at[p, side, :, span(c)],
            zsend.at[p, side, c], zrecv.at[p, side, c],
            "pz", (after, before)[side]["pz"],
        )

    def y_copy(t, side, c):
        p = lax.rem(t, 2)
        return remote(
            field.at[p, (rows_y, 1)[side], inner(c)],
            field.at[p, (0, rows_y + 1)[side], inner(c)],
            ysend.at[p, side, c], yrecv.at[p, side, c],
            "py", (after, before)[side]["py"],
        )

    def x_copy(t, side):
        p = lax.rem(t, 2)
        return remote(
            field.at[p, body_y, (cells, 1)[side]],
            field.at[p, body_y, (0, cells + 1)[side]],
            xsend.at[p, side], xrecv.at[p, side],
            "px", (after, before)[side]["px"],
        )

    def prefix_copy(c):
        return remote(
            running.at[:, span(c), deep - 1], entering.at[:, span(c)],
            psend.at[c], precv.at[c], "pz", after["pz"],
        )

    def x_faces(t, c, act):
        @pl.when(c == 0)
        def _():
            act(x_copy(t, 1))

        @pl.when(c == parts - 1)
        def _():
            act(x_copy(t, 0))

    def send_faces(t, c):
        z_copy(t, 0, c).start()

        @pl.when(jnp.logical_or(t < LAST, mine["pz"] > 0))
        def _():
            z_copy(t, 1, c).start()

        for side in (0, 1):
            y_copy(t, side, c).start()
        x_faces(t, c, lambda copy: copy.start())

    def wait_sent(t, c):
        for side in (0, 1):
            z_copy(t, side, c).wait_send()
            y_copy(t, side, c).wait_send()
        x_faces(t, c, lambda copy: copy.wait_send())

    def wait_faces(t, c):
        for side in (0, 1):
            z_copy(t, side, c).wait_recv()
            y_copy(t, side, c).wait_recv()

        @pl.when(c == 0)
        def _():
            x_copy(t, 0).wait_recv()

        @pl.when(c == parts - 1)
        def _():
            x_copy(t, 1).wait_recv()

    def each(limit, work):
        def run(i, carry):
            work(i)
            return carry

        lax.fori_loop(0, limit, run, 0)

    ahead = min(4, parts)
    for c in range(ahead):
        load(0, c).start()

    barrier = pltpu.get_barrier_semaphore()
    for axis in count:
        for target in (after[axis], before[axis]):
            pl.semaphore_signal(barrier, inc=1, device_id={axis: target}, device_id_type=MESH)
    pl.semaphore_wait(barrier, 6)

    def first_faces(c):
        load(0, c).wait()

        @pl.when(c < parts - ahead)
        def _():
            load(0, c + ahead).start()

        send_faces(0, c)
        load(1, c).start()
        load(2, c).start()

    each(parts, first_faces)

    level = lax.broadcasted_iota(jnp.int32, (wide, deep, members), 1)

    def tall(values):
        return jnp.broadcast_to(values[:, None, :], (wide, deep, members))

    def advanced(p, y, c):
        middle = field[p, y + 1, inner(c)]
        first = tall(zhalo[p, 0, y, span(c)])
        last = tall(zhalo[p, 1, y, span(c)])
        lower = jnp.where(level == 0, first, pltpu.roll(middle, 1, 1))
        upper = jnp.where(level == deep - 1, last, pltpu.roll(middle, deep - 1, 1))
        spread = (
            field[p, y, inner(c)] + field[p, y + 2, inner(c)]
            + field[p, y + 1, inner(c, -1)] + field[p, y + 1, inner(c, 1)]
            + (lower + upper) - 6.0 * middle
        )
        return middle + coeff[y, span(c)] * spread + gain[y, span(c)]

    def step(t, carry):
        old, new = lax.rem(t, 2), lax.rem(t + 1, 2)

        def chunk(c):
            @pl.when(t == 0)
            def _():
                load(1, c).wait()
                load(2, c).wait()

            @pl.when(t > 0)
            def _():
                wait_sent(t - 1, c)

            wait_faces(t, c)

            def row(y):
                field[new, y + 1, inner(c)] = advanced(old, y, c)

            each(rows_y, row)
            send_faces(t + 1, c)

        each(parts, chunk)
        return carry

    lax.fori_loop(0, LAST, step, 0)

    def last_chunk(c):
        wait_faces(LAST, c)

        def row(y):
            block = advanced(LAST % 2, y, c)
            end[y, span(c)] = block
            reach = 1
            while reach < deep:
                block = block + jnp.where(level >= reach, pltpu.roll(block, reach, 1), 0.0)
                reach *= 2
            running[y, span(c)] = block * scale

        each(rows_y, row)

        @pl.when(mine["pz"] > 0)
        def _():
            prefix_copy(c).wait_recv()

            def lift(y):
                running[y, span(c)] = running[y, span(c)] + tall(entering[y, span(c)])

            each(rows_y, lift)

        @pl.when(jnp.logical_not(highest))
        def _():
            prefix_copy(c).start()

        @pl.when(jnp.logical_and(lowest, c >= behind))
        def _():
            z_copy(LAST, 1, c - behind).start()

    each(parts, last_chunk)

    @pl.when(lowest)
    def _():
        each(behind, lambda c: z_copy(LAST, 1, parts - behind + c).start())

    def finish(c):
        wait_sent(LAST - 1, c)
        wait_sent(LAST, c)

        @pl.when(jnp.logical_not(highest))
        def _():
            prefix_copy(c).wait_send()

    each(parts, finish)


def store(end, running, tracer_end, potential, sem):
    rows_y = end.shape[0]
    pieces = next(n for n in (4, 2, 1) if rows_y % n == 0)
    copies = []
    for i in range(pieces):
        part = pl.ds(i * (rows_y // pieces), rows_y // pieces)
        copies.append(pltpu.make_async_copy(end.at[part], tracer_end.at[part], sem.at[0, i]))
        copies.append(pltpu.make_async_copy(running.at[part], potential.at[part], sem.at[1, i]))
    for copy in copies:
        copy.start()
    for copy in copies:
        copy.wait()


def on_device(counts, tracer, conductance, source):
    shape = tracer.shape
    rows_y, cells, deep, members = shape
    parts = chunks_of(cells)
    anywhere = pl.BlockSpec(memory_space=pl.ANY)
    near = pl.BlockSpec(memory_space=pltpu.VMEM)
    f32 = jnp.float32
    dma = pltpu.SemaphoreType.DMA
    end, running = pl.pallas_call(
        functools.partial(evolve, counts, parts),
        out_shape=(pltpu.VMEM(shape, f32), pltpu.VMEM(shape, f32)),
        in_specs=[anywhere] * 3,
        out_specs=(near, near),
        scratch_shapes=[
            pltpu.VMEM((2, rows_y + 2, cells + 2, deep, members), f32),
            pltpu.VMEM(shape, f32),
            pltpu.VMEM(shape, f32),
            pltpu.VMEM((2, 2, rows_y, cells, members), f32),
            pltpu.VMEM((rows_y, cells, members), f32),
            dma((3, parts)),
            dma((2, 2, parts)), dma((2, 2, parts)),
            dma((2, 2, parts)), dma((2, 2, parts)),
            dma((2, 2)), dma((2, 2)),
            dma((parts,)), dma((parts,)),
        ],
        compiler_params=pltpu.CompilerParams(
            collective_id=0, has_side_effects=True, vmem_limit_bytes=44 * 1024 * 1024
        ),
        name="evolve",
    )(tracer, conductance, source)
    tracer_end, potential = pl.pallas_call(
        store,
        out_shape=(jax.ShapeDtypeStruct(shape, f32),) * 2,
        in_specs=[near, near],
        out_specs=(anywhere, anywhere),
        scratch_shapes=[dma((2, 4))],
        compiler_params=pltpu.CompilerParams(vmem_limit_bytes=1024 * 1024),
        name="store",
    )(end, running)
    return potential, tracer_end


def solution(mesh):
    placed = P(*AXES, None)
    counts = tuple(mesh.shape[axis] for axis in AXES)
    return jax.shard_map(
        functools.partial(on_device, counts),
        mesh=mesh,
        in_specs=(placed,) * 3,
        out_specs=(placed,) * 2,
        check_vma=False,
    )
```

time: 223 us -> 224 us (level)
  no operation moved by 1% of the time
where the time goes in v1:
time: 224 us; the launch traced here: 223 us
  Pallas kernels  223 us (100%)
    pallas_call x1, Pallas kernels, on_device(): pl.pallas_call(functools.partial(evolve, counts, parts), out_shape=(pltpu...  217 us
    pallas_call x1, Pallas kernels, on_device(): pl.pallas_call(store, out_shape=(jax.ShapeDtypeStruct(shape, f32),) * 2,...  5.92 us

profile of v1, /device:TPU:24, one launch (start us, length us, event | category | flops | bytes accessed | tf_op | source)
XLA Modules:
  0.0 223.4 jit_solution(6798889206660622820)
XLA Ops:
  0.6 216.8 %evolve.1 = (f32[16,128,8,128]{3,2,1,0:T(8,128)S(1)}, f32[16,128,8,128]{3,2,1,0:T(8,128)S(1)}) custom-call(f32[16,128,8,128]{3,2,1,0:T(8,128)} %tracer.1, f32[16,128,8,128]{3,2,1,0:T(8,128)} %conductance.1, f32[16,128,8,128]{3,2,1,0:T(8,128)} %source.1), custom_call_target="tpu_custom_call" | custom-call | tf_op jit(solution)/shard_map/evolve/pallas_call | solution.py:276
  217.4 5.9 %store.1 = (f32[16,128,8,128]{3,2,1,0:T(8,128)}, f32[16,128,8,128]{3,2,1,0:T(8,128)}) custom-call(f32[16,128,8,128]{3,2,1,0:T(8,128)S(1)} %get-tuple-element.6.end, f32[16,128,8,128]{3,2,1,0:T(8,128)S(1)} %get-tuple-element.7.running), custom_call_target="tpu_custom_call" | custom-call | tf_op jit(solution)/shard_map/store/pallas_call | solution.py:298

commit v2 on v1

--- a/solution.py
+++ b/solution.py
@@ -21,13 +21,18 @@
 
 
 def evolve(
-    counts, parts, tracer, conductance, source, end, running,
+    counts, parts, bands, tracer, conductance, source, end, running,
     field, coeff, gain, zhalo, entering,
     load_sem, zsend, zrecv, ysend, yrecv, xsend, xrecv, psend, precv,
 ):
     rows_y, cells, deep, members = tracer.shape
     wide = cells // parts
-    behind = parts // 2
+    broad = cells // bands
+    per_band = parts // bands
+    ahead = load_sem.shape[0] - 2
+    pieces = precv.shape[0] - parts + 1
+    thick = rows_y // pieces
+    early = parts * 3 // 8
     scale = 1.0 / (deep * counts[2])
     count = dict(zip(AXES, counts))
     mine = {axis: lax.axis_index(axis) for axis in count}
@@ -35,7 +40,9 @@
     before = {axis: lax.rem(mine[axis] + count[axis] - 1, count[axis]) for axis in count}
     lowest = mine["pz"] == 0
     highest = mine["pz"] == count["pz"] - 1
+    held = jnp.clip(count["pz"] - 2 - mine["pz"], 0, 2) * (parts // 4)
     body_y = pl.ds(1, rows_y)
+    body_x = pl.ds(1, cells)
 
     def span(c):
         return pl.ds(pl.multiple_of(c * wide, 8), wide)
@@ -43,13 +50,16 @@
     def inner(c, shift=0):
         return pl.ds(c * wide + 1 + shift, wide)
 
-    def load(which, c):
-        hbm, dst = (
-            (tracer, field.at[0, body_y, inner(c)]),
-            (conductance, coeff.at[:, span(c)]),
-            (source, gain.at[:, span(c)]),
-        )[which]
-        return pltpu.make_async_copy(hbm.at[:, span(c)], dst, load_sem.at[which, c])
+    def load(c):
+        return pltpu.make_async_copy(
+            tracer.at[:, span(c)], field.at[0, body_y, inner(c)], load_sem.at[lax.rem(c, ahead)]
+        )
+
+    def load_rest():
+        return (
+            pltpu.make_async_copy(conductance, coeff, load_sem.at[ahead]),
+            pltpu.make_async_copy(source, gain, load_sem.at[ahead + 1]),
+        )
 
     def remote(src, dst, send, recv, axis, target):
         return pltpu.make_async_remote_copy(
@@ -62,16 +72,31 @@
         return remote(
             field.at[p, body_y, inner(c), (deep - 1, 0)[side]],
             zhalo.at[p, side, :, span(c)],
-            zsend.at[p, side, c], zrecv.at[p, side, c],
+            zsend.at[p, side], zrecv.at[p, c],
             "pz", (after, before)[side]["pz"],
         )
 
-    def y_copy(t, side, c):
-        p = lax.rem(t, 2)
-        return remote(
-            field.at[p, (rows_y, 1)[side], inner(c)],
-            field.at[p, (0, rows_y + 1)[side], inner(c)],
-            ysend.at[p, side, c], yrecv.at[p, side, c],
+    def z_both(t, c):
+        p = lax.rem(t, 2)
+        both = zhalo.at[p, :, :, span(c)]
+        return remote(both, both, zsend.at[p, 0], zrecv.at[p, c], "pz", after["pz"])
+
+    def z_whole(t, side):
+        p = lax.rem(t, 2)
+        return remote(
+            field.at[p, body_y, body_x, (deep - 1, 0)[side]],
+            zhalo.at[p, side],
+            zsend.at[p, side], zrecv.at[p, 0],
+            "pz", (after, before)[side]["pz"],
+        )
+
+    def y_copy(t, side, b, where=None):
+        p = lax.rem(t, 2)
+        where = pl.ds(b * broad + 1, broad) if where is None else where
+        return remote(
+            field.at[p, (rows_y, 1)[side], where],
+            field.at[p, (0, rows_y + 1)[side], where],
+            ysend.at[p, side], yrecv.at[p, side, b],
             "py", (after, before)[side]["py"],
         )
 
@@ -84,42 +109,53 @@
             "px", (after, before)[side]["px"],
         )
 
-    def prefix_copy(c):
-        return remote(
-            running.at[:, span(c), deep - 1], entering.at[:, span(c)],
-            psend.at[c], precv.at[c], "pz", after["pz"],
-        )
-
-    def x_faces(t, c, act):
+    def prefix_copy(c, first, number, recv):
+        part = pl.ds(first, number)
+        return remote(
+            running.at[part, span(c), deep - 1], entering.at[part, span(c)],
+            psend, precv.at[recv], "pz", after["pz"],
+        )
+
+    def prefix_whole():
+        return remote(
+            running.at[:, :, deep - 1], entering, psend, precv.at[0], "pz", after["pz"]
+        )
+
+    def send_faces(t, c):
+        @pl.when((t < LAST) | (c < parts - held))
+        def _():
+            z_copy(t, 0, c).start()
+
+        @pl.when((t < LAST) | (mine["pz"] > 0) | (c < early))
+        def _():
+            z_copy(t, 1, c).start()
+
+        @pl.when(lax.rem(c, per_band) == per_band - 1)
+        def _():
+            for side in (0, 1):
+                y_copy(t, side, lax.div(c, per_band)).start()
+
         @pl.when(c == 0)
         def _():
-            act(x_copy(t, 1))
+            x_copy(t, 1).start()
 
         @pl.when(c == parts - 1)
         def _():
-            act(x_copy(t, 0))
-
-    def send_faces(t, c):
-        z_copy(t, 0, c).start()
-
-        @pl.when(jnp.logical_or(t < LAST, mine["pz"] > 0))
-        def _():
-            z_copy(t, 1, c).start()
-
+            x_copy(t, 0).start()
+
+    def wait_sent(t):
         for side in (0, 1):
-            y_copy(t, side, c).start()
-        x_faces(t, c, lambda copy: copy.start())
-
-    def wait_sent(t, c):
-        for side in (0, 1):
-            z_copy(t, side, c).wait_send()
-            y_copy(t, side, c).wait_send()
-        x_faces(t, c, lambda copy: copy.wait_send())
+            z_whole(t, side).wait_send()
+            y_copy(t, side, 0, body_x).wait_send()
+            x_copy(t, side).wait_send()
 
     def wait_faces(t, c):
-        for side in (0, 1):
-            z_copy(t, side, c).wait_recv()
-            y_copy(t, side, c).wait_recv()
+        z_both(t, c).wait_recv()
+
+        @pl.when(lax.rem(c, per_band) == 0)
+        def _():
+            for side in (0, 1):
+                y_copy(t, side, lax.div(c, per_band)).wait_recv()
 
         @pl.when(c == 0)
         def _():
@@ -136,9 +172,8 @@
 
         lax.fori_loop(0, limit, run, 0)
 
-    ahead = min(4, parts)
     for c in range(ahead):
-        load(0, c).start()
+        load(c).start()
 
     barrier = pltpu.get_barrier_semaphore()
     for axis in count:
@@ -147,17 +182,22 @@
     pl.semaphore_wait(barrier, 6)
 
     def first_faces(c):
-        load(0, c).wait()
+        load(c).wait()
 
         @pl.when(c < parts - ahead)
         def _():
-            load(0, c + ahead).start()
+            load(c + ahead).start()
+
+        @pl.when(c == parts - ahead)
+        def _():
+            for copy in load_rest():
+                copy.start()
 
         send_faces(0, c)
-        load(1, c).start()
-        load(2, c).start()
 
     each(parts, first_faces)
+    for copy in load_rest():
+        copy.wait()
 
     level = lax.broadcasted_iota(jnp.int32, (wide, deep, members), 1)
 
@@ -180,16 +220,11 @@
     def step(t, carry):
         old, new = lax.rem(t, 2), lax.rem(t + 1, 2)
 
+        @pl.when(t > 0)
+        def _():
+            wait_sent(t - 1)
+
         def chunk(c):
-            @pl.when(t == 0)
-            def _():
-                load(1, c).wait()
-                load(2, c).wait()
-
-            @pl.when(t > 0)
-            def _():
-                wait_sent(t - 1, c)
-
             wait_faces(t, c)
 
             def row(y):
@@ -203,7 +238,7 @@
 
     lax.fori_loop(0, LAST, step, 0)
 
-    def last_chunk(c):
+    def finish_chunk(c):
         wait_faces(LAST, c)
 
         def row(y):
@@ -217,38 +252,49 @@
 
         each(rows_y, row)
 
-        @pl.when(mine["pz"] > 0)
-        def _():
-            prefix_copy(c).wait_recv()
-
-            def lift(y):
+    def pass_on(c, first, number, recv):
+        copy = prefix_copy(c, first, number, recv)
+
+        @pl.when(jnp.logical_not(lowest))
+        def _():
+            copy.wait_recv()
+
+            def lift(i):
+                y = first + i
                 running[y, span(c)] = running[y, span(c)] + tall(entering[y, span(c)])
 
-            each(rows_y, lift)
+            each(number, lift)
 
         @pl.when(jnp.logical_not(highest))
         def _():
-            prefix_copy(c).start()
-
-        @pl.when(jnp.logical_and(lowest, c >= behind))
-        def _():
-            z_copy(LAST, 1, c - behind).start()
-
-    each(parts, last_chunk)
-
-    @pl.when(lowest)
+            copy.start()
+
+    def late_faces(c):
+        @pl.when(c < held)
+        def _():
+            z_copy(LAST, 0, parts - held + c).start()
+
+        @pl.when(lowest & (c >= early))
+        def _():
+            z_copy(LAST, 1, c).start()
+
+    finish_chunk(0)
+
+    def last_chunk(i):
+        finish_chunk(i + 1)
+        pass_on(i, 0, rows_y, i)
+        late_faces(i)
+
+    each(parts - 1, last_chunk)
+    each(pieces, lambda h: pass_on(parts - 1, h * thick, thick, parts - 1 + h))
+    late_faces(parts - 1)
+
+    wait_sent(LAST - 1)
+    wait_sent(LAST)
+
+    @pl.when(jnp.logical_not(highest))
     def _():
-        each(behind, lambda c: z_copy(LAST, 1, parts - behind + c).start())
-
-    def finish(c):
-        wait_sent(LAST - 1, c)
-        wait_sent(LAST, c)
-
-        @pl.when(jnp.logical_not(highest))
-        def _():
-            prefix_copy(c).wait_send()
-
-    each(parts, finish)
+        prefix_whole().wait_send()
 
 
 def store(end, running, tracer_end, potential, sem):
@@ -269,12 +315,14 @@
     shape = tracer.shape
     rows_y, cells, deep, members = shape
     parts = chunks_of(cells)
+    bands = min(4, parts)
+    pieces = next(n for n in (4, 2, 1) if rows_y % n == 0)
     anywhere = pl.BlockSpec(memory_space=pl.ANY)
     near = pl.BlockSpec(memory_space=pltpu.VMEM)
     f32 = jnp.float32
     dma = pltpu.SemaphoreType.DMA
     end, running = pl.pallas_call(
-        functools.partial(evolve, counts, parts),
+        functools.partial(evolve, counts, parts, bands),
         out_shape=(pltpu.VMEM(shape, f32), pltpu.VMEM(shape, f32)),
         in_specs=[anywhere] * 3,
         out_specs=(near, near),
@@ -284,11 +332,11 @@
             pltpu.VMEM(shape, f32),
             pltpu.VMEM((2, 2, rows_y, cells, members), f32),
             pltpu.VMEM((rows_y, cells, members), f32),
-            dma((3, parts)),
-            dma((2, 2, parts)), dma((2, 2, parts)),
-            dma((2, 2, parts)), dma((2, 2, parts)),
+            dma((min(4, parts) + 2,)),
+            dma((2, 2)), dma((2, parts)),
+            dma((2, 2)), dma((2, 2, bands)),
             dma((2, 2)), dma((2, 2)),
-            dma((parts,)), dma((parts,)),
+            dma(()), dma((parts - 1 + pieces,)),
         ],
         compiler_params=pltpu.CompilerParams(
             collective_id=0, has_side_effects=True, vmem_limit_bytes=44 * 1024 * 1024

time: 224 us -> 219 us (0.978)
  Pallas kernels: 223 us -> 218 us
    pallas_call x1, Pallas kernels: 217 us -> 212 us  [on_device(): pl.pallas_call(functools.partial(evolve, counts, parts, bands), out_shape...]
where the time goes in v2:
time: 219 us
  Pallas kernels  218 us (100%)
    pallas_call x1, Pallas kernels, on_device(): pl.pallas_call(functools.partial(evolve, counts, parts, bands), out_shape...  212 us
    pallas_call x1, Pallas kernels, on_device(): pl.pallas_call(store, out_shape=(jax.ShapeDtypeStruct(shape, f32),) * 2,...  5.92 us

profile of v2, /device:TPU:24, one launch (start us, length us, event | category | flops | bytes accessed | tf_op | source)
XLA Modules:
  0.0 218.7 jit_solution(7702399771075755046)
XLA Ops:
  0.6 212.1 %evolve.1 = (f32[16,128,8,128]{3,2,1,0:T(8,128)S(1)}, f32[16,128,8,128]{3,2,1,0:T(8,128)S(1)}) custom-call(f32[16,128,8,128]{3,2,1,0:T(8,128)} %tracer.1, f32[16,128,8,128]{3,2,1,0:T(8,128)} %conductance.1, f32[16,128,8,128]{3,2,1,0:T(8,128)} %source.1), custom_call_target="tpu_custom_call" | custom-call | tf_op jit(solution)/shard_map/evolve/pallas_call | solution.py:324
  212.7 5.9 %store.1 = (f32[16,128,8,128]{3,2,1,0:T(8,128)}, f32[16,128,8,128]{3,2,1,0:T(8,128)}) custom-call(f32[16,128,8,128]{3,2,1,0:T(8,128)S(1)} %get-tuple-element.6.end, f32[16,128,8,128]{3,2,1,0:T(8,128)S(1)} %get-tuple-element.7.running), custom_call_target="tpu_custom_call" | custom-call | tf_op jit(solution)/shard_map/store/pallas_call | solution.py:346

commit v3 on v2

--- a/solution.py
+++ b/solution.py
@@ -9,6 +9,12 @@
 
 STEPS = 4
 LAST = STEPS - 1
+EARLY = 6
+HOLD = 4
+FINE = 3
+LEAD = 6
+LAG0 = 1
+LAG1 = 0
 AXES = ("py", "px", "pz")
 MESH = pl.DeviceIdType.MESH
 
@@ -21,8 +27,8 @@
 
 
 def evolve(
-    counts, parts, bands, tracer, conductance, source, end, running,
-    field, coeff, gain, zhalo, entering,
+    counts, parts, bands, pieces, tracer, conductance, source, end, running,
+    field, coeff, gain, zhalo, entering, leaving,
     load_sem, zsend, zrecv, ysend, yrecv, xsend, xrecv, psend, precv,
 ):
     rows_y, cells, deep, members = tracer.shape
@@ -30,9 +36,11 @@
     broad = cells // bands
     per_band = parts // bands
     ahead = load_sem.shape[0] - 2
-    pieces = precv.shape[0] - parts + 1
     thick = rows_y // pieces
-    early = parts * 3 // 8
+    coarse = parts - (precv.shape[0] - parts) // (pieces - 1)
+    early = parts * EARLY // 16
+    lead = parts * LEAD // 16
+    lag = jnp.where(lax.rem(lax.axis_index('px'), 2) == 0, LAG0, LAG1)
     scale = 1.0 / (deep * counts[2])
     count = dict(zip(AXES, counts))
     mine = {axis: lax.axis_index(axis) for axis in count}
@@ -40,7 +48,7 @@
     before = {axis: lax.rem(mine[axis] + count[axis] - 1, count[axis]) for axis in count}
     lowest = mine["pz"] == 0
     highest = mine["pz"] == count["pz"] - 1
-    held = jnp.clip(count["pz"] - 2 - mine["pz"], 0, 2) * (parts // 4)
+    held = jnp.clip(count["pz"] - 2 - mine["pz"], 0, 2) * (parts * HOLD // 16)
     body_y = pl.ds(1, rows_y)
     body_x = pl.ds(1, cells)
 
@@ -112,21 +120,19 @@
     def prefix_copy(c, first, number, recv):
         part = pl.ds(first, number)
         return remote(
-            running.at[part, span(c), deep - 1], entering.at[part, span(c)],
+            leaving.at[part, span(c)], entering.at[part, span(c)],
             psend, precv.at[recv], "pz", after["pz"],
         )
 
     def prefix_whole():
-        return remote(
-            running.at[:, :, deep - 1], entering, psend, precv.at[0], "pz", after["pz"]
-        )
-
-    def send_faces(t, c):
+        return remote(leaving, entering, psend, precv.at[0], "pz", after["pz"])
+
+    def send_faces(t, c, wrap=True):
         @pl.when((t < LAST) | (c < parts - held))
         def _():
             z_copy(t, 0, c).start()
 
-        @pl.when((t < LAST) | (mine["pz"] > 0) | (c < early))
+        @pl.when(((t < LAST) & wrap) | (mine["pz"] > 0) | ((t == LAST) & (c < early)))
         def _():
             z_copy(t, 1, c).start()
 
@@ -176,10 +182,26 @@
         load(c).start()
 
     barrier = pltpu.get_barrier_semaphore()
-    for axis in count:
-        for target in (after[axis], before[axis]):
-            pl.semaphore_signal(barrier, inc=1, device_id={axis: target}, device_id_type=MESH)
-    pl.semaphore_wait(barrier, 6)
+
+    def greet(axis, target):
+        pl.semaphore_signal(barrier, inc=1, device_id={axis: target}, device_id_type=MESH)
+
+    for axis in ("pz", "px", "py"):
+        pl.when((axis != "pz") | jnp.logical_not(highest))(lambda: greet(axis, after[axis]))
+        pl.when((axis != "pz") | jnp.logical_not(lowest))(lambda: greet(axis, before[axis]))
+
+    @pl.when(lowest)
+    def _():
+        pl.semaphore_wait(barrier, 5)
+        greet("pz", before["pz"])
+
+    @pl.when(jnp.logical_not(lowest))
+    def _():
+        pl.semaphore_wait(barrier, 6)
+
+    @pl.when(highest)
+    def _():
+        greet("pz", after["pz"])
 
     def first_faces(c):
         load(c).wait()
@@ -193,7 +215,12 @@
             for copy in load_rest():
                 copy.start()
 
-        send_faces(0, c)
+        send_faces(0, c, c >= lead)
+
+        @pl.when(lowest & (c == lead - 1))
+        def _():
+            pl.semaphore_wait(barrier, 1)
+            each(lead, lambda k: z_copy(0, 1, k).start())
 
     each(parts, first_faces)
     for copy in load_rest():
@@ -248,46 +275,85 @@
             while reach < deep:
                 block = block + jnp.where(level >= reach, pltpu.roll(block, reach, 1), 0.0)
                 reach *= 2
-            running[y, span(c)] = block * scale
+            block = block * scale
+            running[y, span(c)] = block
+            leaving[y, span(c)] = block[:, deep - 1, :]
 
         each(rows_y, row)
 
     def pass_on(c, first, number, recv):
         copy = prefix_copy(c, first, number, recv)
 
+        def rows(work):
+            each(number, lambda i: work(first + i))
+
         @pl.when(jnp.logical_not(lowest))
         def _():
             copy.wait_recv()
 
-            def lift(i):
-                y = first + i
+        @pl.when(jnp.logical_not(lowest | highest))
+        def _():
+            def add(y):
+                leaving[y, span(c)] = leaving[y, span(c)] + entering[y, span(c)]
+
+            rows(add)
+
+        @pl.when(jnp.logical_not(highest))
+        def _():
+            copy.start()
+
+        @pl.when(jnp.logical_not(lowest))
+        def _():
+            def lift(y):
                 running[y, span(c)] = running[y, span(c)] + tall(entering[y, span(c)])
 
-            each(number, lift)
-
-        @pl.when(jnp.logical_not(highest))
-        def _():
-            copy.start()
-
-    def late_faces(c):
+            rows(lift)
+
+    def wrap_part(c, first, number):
+        p = LAST % 2
+
+        @pl.when(lowest & (c >= early))
+        def _():
+            remote(
+                field.at[p, pl.ds(first + 1, number), inner(c), 0],
+                zhalo.at[p, 1, pl.ds(first, number), span(c)],
+                zsend.at[p, 1], zrecv.at[p, c], "pz", before["pz"],
+            ).start()
+
+    finish_chunk(0)
+
+    def coarse_chunk(c):
+        finish_chunk(c + 1)
+        pass_on(c, 0, rows_y, c)
+
         @pl.when(c < held)
         def _():
             z_copy(LAST, 0, parts - held + c).start()
 
-        @pl.when(lowest & (c >= early))
-        def _():
-            z_copy(LAST, 1, c).start()
-
-    finish_chunk(0)
-
-    def last_chunk(i):
-        finish_chunk(i + 1)
-        pass_on(i, 0, rows_y, i)
-        late_faces(i)
-
-    each(parts - 1, last_chunk)
-    each(pieces, lambda h: pass_on(parts - 1, h * thick, thick, parts - 1 + h))
-    late_faces(parts - 1)
+        wrap_part(c - lag, 0, rows_y)
+
+    each(coarse, coarse_chunk)
+
+    def fine_chunk(j):
+        c = coarse + j
+        more = c < parts - 1
+
+        @pl.when(more & jnp.logical_not(highest))
+        def _():
+            finish_chunk(c + 1)
+
+        def piece(h):
+            pass_on(c, h * thick, thick, coarse + j * pieces + h)
+            wrap_part(c - lag, h * thick, thick)
+
+        each(pieces, piece)
+
+        @pl.when(more & highest)
+        def _():
+            finish_chunk(c + 1)
+
+    each(parts - coarse, fine_chunk)
+    each(lag, lambda i: wrap_part(parts - lag + i, 0, rows_y))
 
     wait_sent(LAST - 1)
     wait_sent(LAST)
@@ -298,16 +364,14 @@
 
 
 def store(end, running, tracer_end, potential, sem):
-    rows_y = end.shape[0]
-    pieces = next(n for n in (4, 2, 1) if rows_y % n == 0)
-    copies = []
-    for i in range(pieces):
-        part = pl.ds(i * (rows_y // pieces), rows_y // pieces)
-        copies.append(pltpu.make_async_copy(end.at[part], tracer_end.at[part], sem.at[0, i]))
-        copies.append(pltpu.make_async_copy(running.at[part], potential.at[part], sem.at[1, i]))
-    for copy in copies:
-        copy.start()
-    for copy in copies:
+    whole = (
+        pltpu.make_async_copy(end, tracer_end, sem.at[0]),
+        pltpu.make_async_copy(running, potential, sem.at[1]),
+    )
+    for y in range(end.shape[0]):
+        pltpu.make_async_copy(end.at[y], tracer_end.at[y], sem.at[0]).start()
+        pltpu.make_async_copy(running.at[y], potential.at[y], sem.at[1]).start()
+    for copy in whole:
         copy.wait()
 
 
@@ -322,7 +386,7 @@
     f32 = jnp.float32
     dma = pltpu.SemaphoreType.DMA
     end, running = pl.pallas_call(
-        functools.partial(evolve, counts, parts, bands),
+        functools.partial(evolve, counts, parts, bands, pieces),
         out_shape=(pltpu.VMEM(shape, f32), pltpu.VMEM(shape, f32)),
         in_specs=[anywhere] * 3,
         out_specs=(near, near),
@@ -332,14 +396,15 @@
             pltpu.VMEM(shape, f32),
             pltpu.VMEM((2, 2, rows_y, cells, members), f32),
             pltpu.VMEM((rows_y, cells, members), f32),
+            pltpu.VMEM((rows_y, cells, members), f32),
             dma((min(4, parts) + 2,)),
             dma((2, 2)), dma((2, parts)),
             dma((2, 2)), dma((2, 2, bands)),
             dma((2, 2)), dma((2, 2)),
-            dma(()), dma((parts - 1 + pieces,)),
+            dma(()), dma((parts + FINE * (pieces - 1),)),
         ],
         compiler_params=pltpu.CompilerParams(
-            collective_id=0, has_side_effects=True, vmem_limit_bytes=44 * 1024 * 1024
+            collective_id=0, has_side_effects=True, vmem_limit_bytes=46 * 1024 * 1024
         ),
         name="evolve",
     )(tracer, conductance, source)
@@ -348,7 +413,7 @@
         out_shape=(jax.ShapeDtypeStruct(shape, f32),) * 2,
         in_specs=[near, near],
         out_specs=(anywhere, anywhere),
-        scratch_shapes=[dma((2, 4))],
+        scratch_shapes=[dma((2,))],
         compiler_params=pltpu.CompilerParams(vmem_limit_bytes=1024 * 1024),
         name="store",
     )(end, running)

time: 219 us -> 217 us (level)
  no operation moved by 1% of the time
where the time goes in v3:
time: 217 us; the launch traced here: 216 us
  Pallas kernels  216 us (100%)
    pallas_call x1, Pallas kernels, on_device(): pl.pallas_call(functools.partial(evolve, counts, parts, bands, pieces), o...  210 us
    pallas_call x1, Pallas kernels, on_device(): pl.pallas_call(store, out_shape=(jax.ShapeDtypeStruct(shape, f32),) * 2,...  5.81 us

profile of v3, /device:TPU:24, one launch (start us, length us, event | category | flops | bytes accessed | tf_op | source)
XLA Modules:
  0.0 216.4 jit_solution(12495590760601857465)
XLA Ops:
  0.6 210.0 %evolve.1 = (f32[16,128,8,128]{3,2,1,0:T(8,128)S(1)}, f32[16,128,8,128]{3,2,1,0:T(8,128)S(1)}) custom-call(f32[16,128,8,128]{3,2,1,0:T(8,128)} %tracer.1, f32[16,128,8,128]{3,2,1,0:T(8,128)} %conductance.1, f32[16,128,8,128]{3,2,1,0:T(8,128)} %source.1), custom_call_target="tpu_custom_call" | custom-call | tf_op jit(solution)/shard_map/evolve/pallas_call | solution.py:388
  210.6 5.8 %store.1 = (f32[16,128,8,128]{3,2,1,0:T(8,128)}, f32[16,128,8,128]{3,2,1,0:T(8,128)}) custom-call(f32[16,128,8,128]{3,2,1,0:T(8,128)S(1)} %get-tuple-element.6.end, f32[16,128,8,128]{3,2,1,0:T(8,128)S(1)} %get-tuple-element.7.running), custom_call_target="tpu_custom_call" | custom-call | tf_op jit(solution)/shard_map/store/pallas_call | solution.py:411

commit v4 on v3

--- a/solution.py
+++ b/solution.py
@@ -12,6 +12,8 @@
 EARLY = 6
 HOLD = 4
 FINE = 3
+PIECES = 4
+BANDS = 2
 LEAD = 6
 LAG0 = 1
 LAG1 = 0
@@ -75,19 +77,24 @@
             device_id={axis: target}, device_id_type=MESH,
         )
 
+    paired = max(parts - 4, 0)
+
+    def z_slot(c):
+        return jnp.where(c < paired, lax.div(c, 2), c - paired // 2)
+
     def z_copy(t, side, c):
         p = lax.rem(t, 2)
         return remote(
             field.at[p, body_y, inner(c), (deep - 1, 0)[side]],
             zhalo.at[p, side, :, span(c)],
-            zsend.at[p, side], zrecv.at[p, c],
+            zsend.at[p, side], zrecv.at[p, z_slot(c)],
             "pz", (after, before)[side]["pz"],
         )
 
-    def z_both(t, c):
+    def z_both(t, c, chunks):
         p = lax.rem(t, 2)
-        both = zhalo.at[p, :, :, span(c)]
-        return remote(both, both, zsend.at[p, 0], zrecv.at[p, c], "pz", after["pz"])
+        both = zhalo.at[p, :, :, pl.ds(pl.multiple_of(c * wide, 8), chunks * wide)]
+        return remote(both, both, zsend.at[p, 0], zrecv.at[p, z_slot(c)], "pz", after["pz"])
 
     def z_whole(t, side):
         p = lax.rem(t, 2)
@@ -156,7 +163,14 @@
             x_copy(t, side).wait_send()
 
     def wait_faces(t, c):
-        z_both(t, c).wait_recv()
+        @pl.when(c >= paired)
+        def _():
+            z_both(t, c, 1).wait_recv()
+
+        if paired:
+            @pl.when((c < paired) & (lax.rem(c, 2) == 0))
+            def _():
+                z_both(t, c, 2).wait_recv()
 
         @pl.when(lax.rem(c, per_band) == 0)
         def _():
@@ -312,12 +326,12 @@
     def wrap_part(c, first, number):
         p = LAST % 2
 
-        @pl.when(lowest & (c >= early))
+        @pl.when(lowest & (c >= early) & (c < parts))
         def _():
             remote(
                 field.at[p, pl.ds(first + 1, number), inner(c), 0],
                 zhalo.at[p, 1, pl.ds(first, number), span(c)],
-                zsend.at[p, 1], zrecv.at[p, c], "pz", before["pz"],
+                zsend.at[p, 1], zrecv.at[p, z_slot(c)], "pz", before["pz"],
             ).start()
 
     finish_chunk(0)
@@ -379,8 +393,8 @@
     shape = tracer.shape
     rows_y, cells, deep, members = shape
     parts = chunks_of(cells)
-    bands = min(4, parts)
-    pieces = next(n for n in (4, 2, 1) if rows_y % n == 0)
+    bands = min(BANDS, parts)
+    pieces = next(n for n in (PIECES, 4, 2, 1) if rows_y % n == 0)
     anywhere = pl.BlockSpec(memory_space=pl.ANY)
     near = pl.BlockSpec(memory_space=pltpu.VMEM)
     f32 = jnp.float32
@@ -398,7 +412,7 @@
             pltpu.VMEM((rows_y, cells, members), f32),
             pltpu.VMEM((rows_y, cells, members), f32),
             dma((min(4, parts) + 2,)),
-            dma((2, 2)), dma((2, parts)),
+            dma((2, 2)), dma((2, parts - max(parts - 4, 0) // 2)),
             dma((2, 2)), dma((2, 2, bands)),
             dma((2, 2)), dma((2, 2)),
             dma(()), dma((parts + FINE * (pieces - 1),)),

time: 217 us -> 216 us (level)
  no operation moved by 1% of the time
where the time goes in v4:
time: 216 us
  Pallas kernels  216 us (100%)
    pallas_call x1, Pallas kernels, on_device(): pl.pallas_call(functools.partial(evolve, counts, parts, bands, pieces), o...  210 us
    pallas_call x1, Pallas kernels, on_device(): pl.pallas_call(store, out_shape=(jax.ShapeDtypeStruct(shape, f32),) * 2,...  5.81 us

profile of v4, /device:TPU:24, one launch (start us, length us, event | category | flops | bytes accessed | tf_op | source)
XLA Modules:
  0.0 216.3 jit_solution(5129256560085825468)
XLA Ops:
  0.6 209.8 %evolve.1 = (f32[16,128,8,128]{3,2,1,0:T(8,128)S(1)}, f32[16,128,8,128]{3,2,1,0:T(8,128)S(1)}) custom-call(f32[16,128,8,128]{3,2,1,0:T(8,128)} %tracer.1, f32[16,128,8,128]{3,2,1,0:T(8,128)} %conductance.1, f32[16,128,8,128]{3,2,1,0:T(8,128)} %source.1), custom_call_target="tpu_custom_call" | custom-call | tf_op jit(solution)/shard_map/evolve/pallas_call | solution.py:402
  210.4 5.8 %store.1 = (f32[16,128,8,128]{3,2,1,0:T(8,128)}, f32[16,128,8,128]{3,2,1,0:T(8,128)}) custom-call(f32[16,128,8,128]{3,2,1,0:T(8,128)S(1)} %get-tuple-element.6.end, f32[16,128,8,128]{3,2,1,0:T(8,128)S(1)} %get-tuple-element.7.running), custom_call_target="tpu_custom_call" | custom-call | tf_op jit(solution)/shard_map/store/pallas_call | solution.py:425
